TPU v7x, 32 devices: a whole 2x2x4 slice. The times are simulated.
32 devices in a mesh: batch: 8 (over y, x, core), cols: 4 (over z).
Axes of the slice: x: 2, y: 2, z: 4, core: 2. Of those that a mesh axis runs over, the one named last changes fastest.
Arguments:
- grad_up: float32 [8, 1024, 4096], P('batch', None, 'cols'), may hold values from -0.875 to 0.875
- grad_down: float32 [8, 4096, 1024], P('batch', 'cols'), may hold values from -0.875 to 0.875
- grad_query: float32 [8, 1024, 1024], P('batch', None, 'cols'), may hold values from -0.875 to 0.875
- grad_key: float32 [8, 1024, 1024], P('batch', None, 'cols'), may hold values from -0.875 to 0.875
- grad_value: float32 [8, 1024, 1024], P('batch', None, 'cols'), may hold values from -0.875 to 0.875
- grad_mixed: float32 [8, 1024, 1024], P('batch', 'cols'), may hold values from -0.875 to 0.875
- grad_norm: float32 [8, 1024], P('batch'), may hold values from -8 to 8
- weight_up: float32 [1024, 4096], P('batch', 'cols'), may hold values from -0.1875 to 0.1875
- weight_down: float32 [4096, 1024], P('cols', 'batch'), may hold values from -0.09375 to 0.09375
- weight_query: float32 [1024, 1024], P('batch', 'cols'), may hold values from -0.1875 to 0.1875
- weight_key: float32 [1024, 1024], P('batch', 'cols'), may hold values from -0.1875 to 0.1875
- weight_value: float32 [1024, 1024], P('batch', 'cols'), may hold values from -0.1875 to 0.1875
- weight_mixed: float32 [1024, 1024], P('cols', 'batch'), may hold values from -0.1875 to 0.1875
- weight_norm: float32 [1024], P('batch'), may hold values from 0.25 to 1.75
- moment_up: float32 [1024, 4096], P('batch', 'cols'), may hold values from -1.75 to 1.75
- moment_down: float32 [4096, 1024], P('cols', 'batch'), may hold values from -1.75 to 1.75
- moment_query: float32 [1024, 1024], P('batch', 'cols'), may hold values from -1.75 to 1.75
- moment_key: float32 [1024, 1024], P('batch', 'cols'), may hold values from -1.75 to 1.75
- moment_value: float32 [1024, 1024], P('batch', 'cols'), may hold values from -1.75 to 1.75
- moment_mixed: float32 [1024, 1024], P('cols', 'batch'), may hold values from -1.75 to 1.75
- moment_norm: float32 [1024], P('batch'), may hold values from -1.75 to 1.75
Outputs:
- copy_up: bfloat16 [1024, 4096], P(None, 'cols')
- copy_down: bfloat16 [4096, 1024], P('cols')
- copy_query: bfloat16 [1024, 1024], P(None, 'cols')
- copy_key: bfloat16 [1024, 1024], P(None, 'cols')
- copy_value: bfloat16 [1024, 1024], P(None, 'cols')
- copy_mixed: bfloat16 [1024, 1024], P('cols')
- copy_norm: bfloat16 [1024], replicated
- new_up: float32 [1024, 4096], P('batch', 'cols')
- new_down: float32 [4096, 1024], P('cols', 'batch')
- new_query: float32 [1024, 1024], P('batch', 'cols')
- new_key: float32 [1024, 1024], P('batch', 'cols')
- new_value: float32 [1024, 1024], P('batch', 'cols')
- new_mixed: float32 [1024, 1024], P('cols', 'batch')
- new_norm: float32 [1024], P('batch')
- state_new_up: float32 [1024, 4096], P('batch', 'cols')
- state_new_down: float32 [4096, 1024], P('cols', 'batch')
- state_new_query: float32 [1024, 1024], P('batch', 'cols')
- state_new_key: float32 [1024, 1024], P('batch', 'cols')
- state_new_value: float32 [1024, 1024], P('batch', 'cols')
- state_new_mixed: float32 [1024, 1024], P('cols', 'batch')
- state_new_norm: float32 [1024], P('batch')
All inputs are finite; a program needn't handle non-finite values.
Results may differ from a plain program's by a relative error of at most 0.008.
Values may be sent and summed in bfloat16 or wider, within the bound.
A program may use at most 64 MiB of HBM per device.

v0:
```python
import jax
import jax.numpy as jnp
from jax import lax
from jax.sharding import PartitionSpec as P

learn_rate = 0.1
hold_rate = 0.7


def body(
    grad_up,
    grad_down,
    grad_query,
    grad_key,
    grad_value,
    grad_mixed,
    grad_norm,
    weight_up,
    weight_down,
    weight_query,
    weight_key,
    weight_value,
    weight_mixed,
    weight_norm,
    moment_up,
    moment_down,
    moment_query,
    moment_key,
    moment_value,
    moment_mixed,
    moment_norm,
):
    mean_up, mean_down, mean_query, mean_key, mean_value, mean_mixed = (
        lax.psum_scatter(
            grad_up[0].astype(jnp.bfloat16), "batch", scatter_dimension=0, tiled=True
        ).astype(jnp.float32),
        lax.psum_scatter(
            grad_down[0].astype(jnp.bfloat16), "batch", scatter_dimension=1, tiled=True
        ).astype(jnp.float32),
        lax.psum_scatter(
            grad_query[0].astype(jnp.bfloat16), "batch", scatter_dimension=0, tiled=True
        ).astype(jnp.float32),
        lax.psum_scatter(
            grad_key[0].astype(jnp.bfloat16), "batch", scatter_dimension=0, tiled=True
        ).astype(jnp.float32),
        lax.psum_scatter(
            grad_value[0].astype(jnp.bfloat16), "batch", scatter_dimension=0, tiled=True
        ).astype(jnp.float32),
        lax.psum_scatter(
            grad_mixed[0].astype(jnp.bfloat16), "batch", scatter_dimension=1, tiled=True
        ).astype(jnp.float32),
    )
    whole_norm = lax.psum(grad_norm[0], "batch")
    place = lax.axis_index("batch")
    mean_norm = lax.dynamic_slice_in_dim(
        whole_norm, place * weight_norm.shape[0], weight_norm.shape[0]
    )
    mean_rate = lax.axis_size("batch") ** (-0.5)
    mean_up = mean_up * mean_rate
    mean_down = mean_down * mean_rate
    mean_query = mean_query * mean_rate
    mean_key = mean_key * mean_rate
    mean_value = mean_value * mean_rate
    mean_mixed = mean_mixed * mean_rate
    mean_norm = mean_norm * mean_rate
    state_new_up = hold_rate * moment_up + mean_up
    new_up = weight_up - learn_rate * state_new_up
    state_new_down = hold_rate * moment_down + mean_down
    new_down = weight_down - learn_rate * state_new_down
    state_new_query = hold_rate * moment_query + mean_query
    new_query = weight_query - learn_rate * state_new_query
    state_new_key = hold_rate * moment_key + mean_key
    new_key = weight_key - learn_rate * state_new_key
    state_new_value = hold_rate * moment_value + mean_value
    new_value = weight_value - learn_rate * state_new_value
    state_new_mixed = hold_rate * moment_mixed + mean_mixed
    new_mixed = weight_mixed - learn_rate * state_new_mixed
    state_new_norm = hold_rate * moment_norm + mean_norm
    new_norm = weight_norm - learn_rate * state_new_norm
    copy_up, copy_down, copy_query, copy_key, copy_value, copy_mixed, copy_norm = (
        lax.all_gather(new_up.astype(jnp.bfloat16), "batch", axis=0, tiled=True),
        lax.all_gather(new_down.astype(jnp.bfloat16), "batch", axis=1, tiled=True),
        lax.all_gather(new_query.astype(jnp.bfloat16), "batch", axis=0, tiled=True),
        lax.all_gather(new_key.astype(jnp.bfloat16), "batch", axis=0, tiled=True),
        lax.all_gather(new_value.astype(jnp.bfloat16), "batch", axis=0, tiled=True),
        lax.all_gather(new_mixed.astype(jnp.bfloat16), "batch", axis=1, tiled=True),
        lax.all_gather(new_norm.astype(jnp.bfloat16), "batch", axis=0, tiled=True),
    )
    return (
        copy_up,
        copy_down,
        copy_query,
        copy_key,
        copy_value,
        copy_mixed,
        copy_norm,
        new_up,
        new_down,
        new_query,
        new_key,
        new_value,
        new_mixed,
        new_norm,
        state_new_up,
        state_new_down,
        state_new_query,
        state_new_key,
        state_new_value,
        state_new_mixed,
        state_new_norm,
    )


def solution(mesh):
    in_specs = (
        P("batch", None, "cols"),
        P("batch", "cols", None),
        P("batch", None, "cols"),
        P("batch", None, "cols"),
        P("batch", None, "cols"),
        P("batch", "cols", None),
        P("batch", None),
        P("batch", "cols"),
        P("cols", "batch"),
        P("batch", "cols"),
        P("batch", "cols"),
        P("batch", "cols"),
        P("cols", "batch"),
        P("batch"),
        P("batch", "cols"),
        P("cols", "batch"),
        P("batch", "cols"),
        P("batch", "cols"),
        P("batch", "cols"),
        P("cols", "batch"),
        P("batch"),
    )
    out_specs = (
        P(None, "cols"),
        P("cols", None),
        P(None, "cols"),
        P(None, "cols"),
        P(None, "cols"),
        P("cols", None),
        P(),
        P("batch", "cols"),
        P("cols", "batch"),
        P("batch", "cols"),
        P("batch", "cols"),
        P("batch", "cols"),
        P("cols", "batch"),
        P("batch"),
        P("batch", "cols"),
        P("cols", "batch"),
        P("batch", "cols"),
        P("batch", "cols"),
        P("batch", "cols"),
        P("cols", "batch"),
        P("batch"),
    )
    return jax.shard_map(body, mesh=mesh, in_specs=in_specs, out_specs=out_specs, check_vma=False)
```

profile of v0, /device:TPU:0, one launch (start us, length us, event | category | flops | bytes accessed | tf_op | source)
XLA Modules:
  0.0 326.9 jit_solution(14137713241253828921)
XLA Ops:
  7.2 3.8 %convert_bitcast_fusion.1 = bf16[1024,1024]{1,0:T(8,128)(2,1)} fusion(f32[1,1024,1024]{2,1,0:T(8,128)} %param.21), kind=kLoop, calls=%fused_computation.1 | loop fusion | flops 1048576 | bytes 6291456 | tf_op jit(solution)/shard_map/convert_element_type | solution.py:35
  11.1 2.5 convert_bitcast_fusion
  13.7 2.6 copy.42
  16.3 1.1 copy-done.1
  17.5 0.8 convert_bitcast_fusion.5
  18.4 0.8 convert_bitcast_fusion.4
  19.3 0.8 convert_bitcast_fusion.3
  20.3 1.0 copy.44
  21.4 34.3 %reduce-scatter.11.cloned.1.call-done = bf16[128,1024]{1,0:T(8,128)(2,1)} async-done(((bf16[1024,1024]{1,0:T(8,128)(2,1)}), bf16[128,1024]{1,0:T(8,128)(2,1)}) %reduce-scatter.11.cloned.1.call-update) | async-done | bytes 262160 | tf_op jit(solution)/shard_map/reduce_scatter | solution.py:34
  55.7 2.1 fusion.5
  58.0 42.7 %reduce-scatter.19.cloned.1.call-done = bf16[128,1024]{1,0:T(8,128)(2,1)} async-done(((bf16[1024,1024]{1,0:T(8,128)(2,1)}), bf16[128,1024]{1,0:T(8,128)(2,1)}) %reduce-scatter.19.cloned.1.call-update) | async-done | bytes 262160
  100.7 1.1 copy.43
  101.9 1.2 fusion.4
  103.1 12.7 %psum.7 = f32[1024]{0:T(1024)S(1)} all-reduce(f32[1024]{0:T(1024)S(1)} %bitcast.24), channel_id=1, replica_groups=mesh['batch'=8,'cols'=4] {'batch'}, use_global_device_ids=true, to_apply=%region_6.0 | all-reduce | flops 1024 | bytes 8192 | tf_op jit(solution)/shard_map/psum | solution.py:53
  116.4 8.7 %all-gather = bf16[8,1,128]{2,1,0:T(2,128)(2,1)S(1)} all-gather(bf16[1,1,128]{2,1,0:T(2,128)(2,1)S(1)} %get-tuple-element.21), channel_id=1, replica_groups=mesh['batch'=8,'cols'=4] {'batch'}, dimensions={0}, use_global_device_ids=true | all-gather | bytes 2304 | tf_op jit(solution)/shard_map/all_gather | solution.py:87
  125.7 12.8 %reduce-scatter.13.cloned.1.call-done = bf16[128,256]{1,0:T(8,128)(2,1)} async-done(((bf16[1024,256]{1,0:T(8,128)(2,1)}), bf16[128,256]{1,0:T(8,128)(2,1)}) %reduce-scatter.13.cloned.1.call-update) | async-done | bytes 65552 | tf_op jit(solution)/shard_map/reduce_scatter | solution.py:40
  138.5 1.6 fusion.3
  140.1 9.8 %all_gather.23 = bf16[1024,256]{1,0:T(8,128)(2,1)S(1)} all-gather(bf16[128,256]{1,0:T(8,128)(2,1)S(1)} %get-tuple-element.33), channel_id=1, replica_groups=mesh['batch'=8,'cols'=4] {'batch'}, dimensions={0}, use_global_device_ids=true | all-gather | bytes 589824 | tf_op jit(solution)/shard_map/all_gather | solution.py:83
  149.9 26.3 %reduce-scatter.15.cloned.1.call-done = bf16[128,256]{1,0:T(8,128)(2,1)} async-done(((bf16[1024,256]{1,0:T(8,128)(2,1)}), bf16[128,256]{1,0:T(8,128)(2,1)}) %reduce-scatter.15.cloned.1.call-update) | async-done | bytes 65552 | tf_op jit(solution)/shard_map/reduce_scatter | solution.py:43
  176.2 1.6 fusion.2
  177.7 9.8 %all_gather.24 = bf16[1024,256]{1,0:T(8,128)(2,1)S(1)} all-gather(bf16[128,256]{1,0:T(8,128)(2,1)S(1)} %get-tuple-element.30), channel_id=1, replica_groups=mesh['batch'=8,'cols'=4] {'batch'}, dimensions={0}, use_global_device_ids=true | all-gather | bytes 589824 | tf_op jit(solution)/shard_map/all_gather | solution.py:84
  187.5 26.3 %reduce-scatter.17.cloned.1.call-done = bf16[128,256]{1,0:T(8,128)(2,1)} async-done(((bf16[1024,256]{1,0:T(8,128)(2,1)}), bf16[128,256]{1,0:T(8,128)(2,1)}) %reduce-scatter.17.cloned.1.call-update) | async-done | bytes 65552 | tf_op jit(solution)/shard_map/reduce_scatter | solution.py:46
  213.8 1.6 fusion.1
  215.4 9.8 %all_gather.25 = bf16[1024,256]{1,0:T(8,128)(2,1)S(1)} all-gather(bf16[128,256]{1,0:T(8,128)(2,1)S(1)} %get-tuple-element.27), channel_id=1, replica_groups=mesh['batch'=8,'cols'=4] {'batch'}, dimensions={0}, use_global_device_ids=true | all-gather | bytes 589824 | tf_op jit(solution)/shard_map/all_gather | solution.py:85
  225.2 26.3 %reduce-scatter.21.cloned.1.call-done = bf16[128,256]{1,0:T(8,128)(2,1)} async-done(((bf16[1024,256]{1,0:T(8,128)(2,1)}), bf16[128,256]{1,0:T(8,128)(2,1)}) %reduce-scatter.21.cloned.1.call-update) | async-done | bytes 65552
  251.5 0.9 copy.45
  253.2 9.9 %all_gather.26 = bf16[256,1024]{1,0:T(8,128)(2,1)S(1)} all-gather(bf16[256,128]{1,0:T(8,128)(2,1)S(1)} %get-tuple-element.24), channel_id=1, replica_groups=mesh['batch'=8,'cols'=4] {'batch'}, dimensions={1}, use_global_device_ids=true | all-gather | bytes 589824 | tf_op jit(solution)/shard_map/all_gather | solution.py:86
  263.1 18.7 %all-gather.4.cloned.1.call-done = bf16[1024,1024]{1,0:T(8,128)(2,1)} async-done(((bf16[128,1024]{1,0:T(8,128)(2,1)}), bf16[1024,1024]{1,0:T(8,128)(2,1)}) %all-gather.4.cloned.1.call-update) | async-done | bytes 2097168 | tf_op jit(solution)/shard_map/all_gather | solution.py:81
  281.8 30.6 %all-gather.6.cloned.1.call-done = bf16[1024,1024]{1,0:T(8,128)(2,1)} async-done(((bf16[1024,128]{1,0:T(8,128)(2,1)}), bf16[1024,1024]{1,0:T(8,128)(2,1)}) %all-gather.6.cloned.1.call-update) | async-done | bytes 2097168 | tf_op jit(solution)/shard_map/all_gather | solution.py:82
  312.4 3.2 copy.52
  315.6 1.3 copy.53
  316.9 0.8 copy.54
  (62 shorter events, 4.9 us)
Async XLA Ops:
  7.2 48.5 %reduce-scatter.11.cloned.1.call-start = ((), (), s32[]{:S(2)}) async-start(), calls=%async_computation.6 | async-start | bytes 2359296 | tf_op jit(solution)/shard_map/reduce_scatter | solution.py:34
  11.1 89.6 %reduce-scatter.19.cloned.1.call-start = ((), (), s32[]{:S(2)}) async-start(), calls=%async_computation.12 | async-start | bytes 2359296
  16.2 1.2 copy-start.1
  16.2 2.2 copy-start.2
  16.3 3.1 copy-start.3
  16.3 122.2 %reduce-scatter.13.cloned.1.call-start = ((), (), s32[]{:S(2)}) async-start(), calls=%async_computation.9 | async-start | bytes 589824 | tf_op jit(solution)/shard_map/reduce_scatter | solution.py:40
  18.3 1.9 copy-start.4
  18.3 157.8 %reduce-scatter.15.cloned.1.call-start = ((), (), s32[]{:S(2)}) async-start(), calls=%async_computation.10 | async-start | bytes 589824 | tf_op jit(solution)/shard_map/reduce_scatter | solution.py:43
  19.3 194.6 %reduce-scatter.17.cloned.1.call-start = ((), (), s32[]{:S(2)}) async-start(), calls=%async_computation.11 | async-start | bytes 589824 | tf_op jit(solution)/shard_map/reduce_scatter | solution.py:46
  20.2 35.6 %copy-start.5 = (f32[128,1024]{1,0:T(8,128)S(1)}, f32[128,1024]{1,0:T(8,128)}, u32[]{:S(2)}) copy-start(f32[128,1024]{1,0:T(8,128)} %param.28) | copy-start | bytes 1572868
  20.2 35.6 %copy-start.6 = (f32[128,1024]{1,0:T(8,128)S(1)}, f32[128,1024]{1,0:T(8,128)}, u32[]{:S(2)}) copy-start(f32[128,1024]{1,0:T(8,128)} %param.35) | copy-start | bytes 1572868
  20.2 231.3 %reduce-scatter.21.cloned.1.call-start = ((), (), s32[]{:S(2)}) async-start(), calls=%async_computation.13 | async-start | bytes 589824
  21.3 80.5 %copy-start.7 = (f32[1024,128]{1,0:T(8,128)S(1)}, f32[1024,128]{1,0:T(8,128)}, u32[]{:S(2)}) copy-start(f32[1024,128]{1,0:T(8,128)} %param.29) | copy-start | bytes 1572868
  21.3 80.5 %copy-start.8 = (f32[1024,128]{1,0:T(8,128)S(1)}, f32[1024,128]{1,0:T(8,128)}, u32[]{:S(2)}) copy-start(f32[1024,128]{1,0:T(8,128)} %param.36) | copy-start | bytes 1572868
  21.4 260.4 %all-gather.4.cloned.1.call-start = ((), (), s32[]{:S(2)}) async-start(), calls=%async_computation.7 | async-start | bytes 2359296 | tf_op jit(solution)/shard_map/all_gather | solution.py:81
  57.9 45.2 %copy-start.17 = (f32[1,1024]{1,0:T(1,128)S(1)}, f32[1,1024]{1,0:T(1,128)}, u32[]{:S(2)}) copy-start(f32[1,1024]{1,0:T(1,128)} %param.27) | copy-start | bytes 12292
  57.9 57.9 %copy-start.18 = (f32[128]{0:T(128)S(1)}, f32[128]{0:T(128)}, u32[]{:S(2)}) copy-start(f32[128]{0:T(128)} %param.34) | copy-start | bytes 1540
  57.9 57.9 %copy-start.19 = (f32[128]{0:T(128)S(1)}, f32[128]{0:T(128)}, u32[]{:S(2)}) copy-start(f32[128]{0:T(128)} %param.41) | copy-start | bytes 1540
  57.9 80.6 %copy-start.9 = (f32[128,256]{1,0:T(8,128)S(1)}, f32[128,256]{1,0:T(8,128)}, u32[]{:S(2)}) copy-start(f32[128,256]{1,0:T(8,128)} %param.30) | copy-start | bytes 393220
  57.9 80.6 %copy-start.10 = (f32[128,256]{1,0:T(8,128)S(1)}, f32[128,256]{1,0:T(8,128)}, u32[]{:S(2)}) copy-start(f32[128,256]{1,0:T(8,128)} %param.37) | copy-start | bytes 393220
  57.9 254.4 %all-gather.6.cloned.1.call-start = ((), (), s32[]{:S(2)}) async-start(), calls=%async_computation.8 | async-start | bytes 2359296 | tf_op jit(solution)/shard_map/all_gather | solution.py:82
  101.9 74.3 %copy-start.11 = (f32[128,256]{1,0:T(8,128)S(1)}, f32[128,256]{1,0:T(8,128)}, u32[]{:S(2)}) copy-start(f32[128,256]{1,0:T(8,128)} %param.31) | copy-start | bytes 393220
  101.9 74.3 %copy-start.12 = (f32[128,256]{1,0:T(8,128)S(1)}, f32[128,256]{1,0:T(8,128)}, u32[]{:S(2)}) copy-start(f32[128,256]{1,0:T(8,128)} %param.38) | copy-start | bytes 393220
  101.9 112.0 %copy-start.13 = (f32[128,256]{1,0:T(8,128)S(1)}, f32[128,256]{1,0:T(8,128)}, u32[]{:S(2)}) copy-start(f32[128,256]{1,0:T(8,128)} %param.32) | copy-start | bytes 393220
  101.9 112.0 %copy-start.14 = (f32[128,256]{1,0:T(8,128)S(1)}, f32[128,256]{1,0:T(8,128)}, u32[]{:S(2)}) copy-start(f32[128,256]{1,0:T(8,128)} %param.39) | copy-start | bytes 393220
  103.1 149.4 %copy-start.15 = (f32[256,128]{1,0:T(8,128)S(1)}, f32[256,128]{1,0:T(8,128)}, u32[]{:S(2)}) copy-start(f32[256,128]{1,0:T(8,128)} %param.33) | copy-start | bytes 393220
  103.1 149.4 %copy-start.16 = (f32[256,128]{1,0:T(8,128)S(1)}, f32[256,128]{1,0:T(8,128)}, u32[]{:S(2)}) copy-start(f32[256,128]{1,0:T(8,128)} %param.40) | copy-start | bytes 393220
  312.4 3.2 copy-start
Sparse Core Ops, SparseCore 0:
  11.9 43.8 reduce-scatter.10
  59.6 41.0 reduce-scatter.18
  104.4 34.0 reduce-scatter.12
  142.0 34.1 reduce-scatter.14
  179.7 34.1 reduce-scatter.16
  217.3 34.1 reduce-scatter.20
  254.0 27.7 all-gather.3
  284.2 28.0 all-gather.5
where the time goes:
time: 327 us
  waiting for transfers between devices  218 us (67%)
  blocking collectives  60.6 us (19%)
  other arithmetic  18.9 us (6%)
  local copies, waits for them, and re-layouts  14.6 us (4%)
  between operations  14.4 us (4%)
    unnamed x10, waiting for transfers between devices  69.2 us
    reduce_scatter x1, waiting for transfers between devices, body(): lax.psum_scatter(grad_up[0].astype(jnp.bfloat16), 'batch', scatter_dimens...  34.3 us
    all_gather x1, waiting for transfers between devices, body(): lax.all_gather(new_down.astype(jnp.bfloat16), 'batch', axis=1, tiled=True)  30.6 us
    reduce_scatter x1, waiting for transfers between devices, body(): lax.psum_scatter(grad_key[0].astype(jnp.bfloat16), 'batch', scatter_dimen...  26.3 us
    reduce_scatter x1, waiting for transfers between devices, body(): lax.psum_scatter(grad_value[0].astype(jnp.bfloat16), 'batch', scatter_dim...  26.3 us
    all_gather x1, waiting for transfers between devices, body(): lax.all_gather(new_up.astype(jnp.bfloat16), 'batch', axis=0, tiled=True)  18.7 us
    unnamed x50, local copies, waits for them, and re-layouts  14.6 us
    reduce_scatter x1, waiting for transfers between devices, body(): lax.psum_scatter(grad_query[0].astype(jnp.bfloat16), 'batch', scatter_dim...  12.8 us
  transfers between devices with their start and end apart: 8, of which 8 were waited for; matrix products, arithmetic and copies ran while one was open for 6% of the time, Pallas kernels for 0%

commit v1 on v0

--- a/solution.py
+++ b/solution.py
@@ -79,7 +79,12 @@
     new_norm = weight_norm - learn_rate * state_new_norm
     copy_up, copy_down, copy_query, copy_key, copy_value, copy_mixed, copy_norm = (
         lax.all_gather(new_up.astype(jnp.bfloat16), "batch", axis=0, tiled=True),
-        lax.all_gather(new_down.astype(jnp.bfloat16), "batch", axis=1, tiled=True),
+        jnp.concatenate(
+            lax.all_to_all(
+                jnp.stack([new_down.astype(jnp.bfloat16)] * lax.axis_size("batch")), "batch", 0, 0
+            ),
+            axis=1,
+        ),
         lax.all_gather(new_query.astype(jnp.bfloat16), "batch", axis=0, tiled=True),
         lax.all_gather(new_key.astype(jnp.bfloat16), "batch", axis=0, tiled=True),
         lax.all_gather(new_value.astype(jnp.bfloat16), "batch", axis=0, tiled=True),

time: 327 us -> 299 us (0.914)
  waiting for transfers between devices: 218 us -> 154 us
  blocking collectives: 60.6 us -> 83.5 us
  local copies, waits for them, and re-layouts: 14.6 us -> 21.2 us
  starting transfers between devices: 0.33 us -> 4.04 us
    all_gather x1 -> x0, waiting for transfers between devices: 30.6 us -> none  [body(): lax.all_gather(new_down.astype(jnp.bfloat16), 'batch', axis=1, tiled=True)]
    psum x1, blocking collectives: 12.7 us -> 34.4 us  [body(): whole_norm = lax.psum(grad_norm[0], 'batch')]
    reduce_scatter x1, waiting for transfers between devices: 12.8 us -> 0.01 us  [body(): lax.psum_scatter(grad_query[0].astype(jnp.bfloat16), 'batch', scatter_dim...]
    reduce_scatter x1, waiting for transfers between devices: 26.3 us -> 16.4 us  [body(): lax.psum_scatter(grad_key[0].astype(jnp.bfloat16), 'batch', scatter_dimen...]
    all_gather x1, waiting for transfers between devices: 18.7 us -> 9.64 us  [body(): lax.all_gather(new_up.astype(jnp.bfloat16), 'batch', axis=0, tiled=True)]
    all_to_all x0 -> x1, starting transfers between devices: none -> 3.75 us  [body(): lax.all_to_all(jnp.stack([new_down.astype(jnp.bfloat16)] * lax.axis_size(...]
    unnamed x50 -> x48, local copies, waits for them, and re-layouts: 14.6 us -> 17 us
    unnamed x10 -> x9, waiting for transfers between devices: 69.2 us -> 68.3 us
  transfers between devices with their start and end apart: 8 -> 8, of which waited for: 8 -> 6; matrix products, arithmetic and copies ran while one was open for 6% -> 10% of each run, Pallas kernels for 0% -> 0%
where the time goes in v1:
time: 299 us; the launch traced here: 298 us
  waiting for transfers between devices  154 us (52%)
  blocking collectives  83.5 us (28%)
  local copies, waits for them, and re-layouts  21.2 us (7%)
  other arithmetic  21.1 us (7%)
  between operations  14.3 us (5%)
  starting transfers between devices  4.04 us (1%)
    unnamed x9, waiting for transfers between devices  68.3 us
    psum x1, blocking collectives, body(): whole_norm = lax.psum(grad_norm[0], 'batch')  34.4 us
    reduce_scatter x1, waiting for transfers between devices, body(): lax.psum_scatter(grad_up[0].astype(jnp.bfloat16), 'batch', scatter_dimens...  33 us
    reduce_scatter x1, waiting for transfers between devices, body(): lax.psum_scatter(grad_value[0].astype(jnp.bfloat16), 'batch', scatter_dim...  26.3 us
    unnamed x48, local copies, waits for them, and re-layouts  17 us
    reduce_scatter x1, waiting for transfers between devices, body(): lax.psum_scatter(grad_key[0].astype(jnp.bfloat16), 'batch', scatter_dimen...  16.4 us
    all_gather x1, blocking collectives, body(): lax.all_gather(new_mixed.astype(jnp.bfloat16), 'batch', axis=1, tiled=True)  10.9 us
    all_gather x1, blocking collectives, body(): lax.all_gather(new_value.astype(jnp.bfloat16), 'batch', axis=0, tiled=True)  10.7 us
  transfers between devices with their start and end apart: 8, of which 6 were waited for; matrix products, arithmetic and copies ran while one was open for 10% of the time, Pallas kernels for 0%

profile of v1, /device:TPU:0, one launch (start us, length us, event | category | flops | bytes accessed | tf_op | source)
XLA Modules:
  0.0 297.8 jit_solution(17572315925445467419)
XLA Ops:
  7.2 3.8 %convert_bitcast_fusion.1 = bf16[1024,1024]{1,0:T(8,128)(2,1)} fusion(f32[1,1024,1024]{2,1,0:T(8,128)} %param.21), kind=kLoop, calls=%fused_computation.1 | loop fusion | flops 1048576 | bytes 6291456 | tf_op jit(solution)/shard_map/convert_element_type | solution.py:35
  11.1 2.5 convert_bitcast_fusion
  13.7 2.6 copy.44
  16.3 1.1 copy-done.2
  19.3 0.8 convert_bitcast_fusion.3
  20.2 1.4 convert_bitcast_fusion.2
  21.6 1.0 copy.46
  22.7 33.0 %reduce-scatter.11.cloned.1.call-done = bf16[128,1024]{1,0:T(8,128)(2,1)} async-done(((bf16[1024,1024]{1,0:T(8,128)(2,1)}), bf16[128,1024]{1,0:T(8,128)(2,1)}) %reduce-scatter.11.cloned.1.call-update) | async-done | bytes 262160 | tf_op jit(solution)/shard_map/reduce_scatter | solution.py:34
  55.7 2.1 fusion.5
  57.9 42.8 %reduce-scatter.19.cloned.1.call-done = bf16[128,1024]{1,0:T(8,128)(2,1)} async-done(((bf16[1024,1024]{1,0:T(8,128)(2,1)}), bf16[128,1024]{1,0:T(8,128)(2,1)}) %reduce-scatter.19.cloned.1.call-update) | async-done | bytes 262160
  100.7 1.1 copy.45
  101.9 1.1 fusion.4
  103.0 1.6 stack.2
  104.6 3.7 %all-to-all-start = ((bf16[8,1024,128]{2,1,0:T(8,128)(2,1)}), bf16[8,1024,128]{2,1,0:T(8,128)(2,1)S(1)}, u32[]{:S(2)}, u32[]{:S(2)}) async-start(bf16[8,1024,128]{2,1,0:T(8,128)(2,1)} %stack.2), calls=%async_computation.1 | async-start | bytes 4194304 | tf_op jit(solution)/shard_map/all_to_all | solution.py:83
  108.4 34.4 %psum.7 = f32[1024]{0:T(1024)S(1)} all-reduce(f32[1024]{0:T(1024)S(1)} %bitcast.28), channel_id=1, replica_groups=mesh['batch'=8,'cols'=4] {'batch'}, use_global_device_ids=true, to_apply=%region_6.0 | all-reduce | flops 1024 | bytes 8192 | tf_op jit(solution)/shard_map/psum | solution.py:53
  143.4 8.9 %all-gather = bf16[8,1,128]{2,1,0:T(2,128)(2,1)S(1)} all-gather(bf16[1,1,128]{2,1,0:T(2,128)(2,1)S(1)} %get-tuple-element.42), channel_id=1, replica_groups=mesh['batch'=8,'cols'=4] {'batch'}, dimensions={0}, use_global_device_ids=true | all-gather | bytes 2304 | tf_op jit(solution)/shard_map/all_gather | solution.py:92
  153.0 1.6 fusion.3
  154.5 8.7 %all_gather.19 = bf16[1024,256]{1,0:T(8,128)(2,1)S(1)} all-gather(bf16[128,256]{1,0:T(8,128)(2,1)S(1)} %get-tuple-element.54), channel_id=1, replica_groups=mesh['batch'=8,'cols'=4] {'batch'}, dimensions={0}, use_global_device_ids=true | all-gather | bytes 589824 | tf_op jit(solution)/shard_map/all_gather | solution.py:88
  163.2 16.4 %reduce-scatter.15.cloned.1.call-done = bf16[128,256]{1,0:T(8,128)(2,1)} async-done(((bf16[1024,256]{1,0:T(8,128)(2,1)}), bf16[128,256]{1,0:T(8,128)(2,1)}) %reduce-scatter.15.cloned.1.call-update) | async-done | bytes 65552 | tf_op jit(solution)/shard_map/reduce_scatter | solution.py:43
  179.7 1.6 fusion.2
  181.2 9.8 %all_gather.20 = bf16[1024,256]{1,0:T(8,128)(2,1)S(1)} all-gather(bf16[128,256]{1,0:T(8,128)(2,1)S(1)} %get-tuple-element.51), channel_id=1, replica_groups=mesh['batch'=8,'cols'=4] {'batch'}, dimensions={0}, use_global_device_ids=true | all-gather | bytes 589824 | tf_op jit(solution)/shard_map/all_gather | solution.py:89
  191.0 26.3 %reduce-scatter.17.cloned.1.call-done = bf16[128,256]{1,0:T(8,128)(2,1)} async-done(((bf16[1024,256]{1,0:T(8,128)(2,1)}), bf16[128,256]{1,0:T(8,128)(2,1)}) %reduce-scatter.17.cloned.1.call-update) | async-done | bytes 65552 | tf_op jit(solution)/shard_map/reduce_scatter | solution.py:46
  217.3 1.6 fusion.1
  218.9 10.7 %all_gather.21 = bf16[1024,256]{1,0:T(8,128)(2,1)} all-gather(bf16[128,256]{1,0:T(8,128)(2,1)S(1)} %get-tuple-element.48), channel_id=1, replica_groups=mesh['batch'=8,'cols'=4] {'batch'}, dimensions={0}, use_global_device_ids=true | all-gather | bytes 589824 | tf_op jit(solution)/shard_map/all_gather | solution.py:90
  229.6 25.3 %reduce-scatter.21.cloned.1.call-done = bf16[128,256]{1,0:T(8,128)(2,1)} async-done(((bf16[1024,256]{1,0:T(8,128)(2,1)}), bf16[128,256]{1,0:T(8,128)(2,1)}) %reduce-scatter.21.cloned.1.call-update) | async-done | bytes 65552
  255.0 0.9 copy.47
  255.9 1.6 fusion
  257.6 10.9 %all_gather.22 = bf16[256,1024]{1,0:T(8,128)(2,1)} all-gather(bf16[256,128]{1,0:T(8,128)(2,1)S(1)} %get-tuple-element.45), channel_id=1, replica_groups=mesh['batch'=8,'cols'=4] {'batch'}, dimensions={1}, use_global_device_ids=true | all-gather | bytes 589824 | tf_op jit(solution)/shard_map/all_gather | solution.py:91
  268.5 2.6 copy.42
  271.1 3.9 %copy.43 = bf16[1024,1024]{1,0:T(8,128)(2,1)} copy(bf16[1024,1024]{0,1:T(8,128)(2,1)} %bitcast.24) | data formatting | bytes 4194304
  275.0 9.6 %all-gather.3.cloned.1.call-done = bf16[1024,1024]{1,0:T(8,128)(2,1)} async-done(((bf16[128,1024]{1,0:T(8,128)(2,1)}), bf16[1024,1024]{1,0:T(8,128)(2,1)}) %all-gather.3.cloned.1.call-update) | async-done | bytes 2097168 | tf_op jit(solution)/shard_map/all_gather | solution.py:81
  284.7 3.1 %copy.53 = bf16[1024,1024]{1,0:T(8,128)(2,1)} copy(bf16[1024,1024]{1,0:T(8,128)(2,1)} %all-gather.3.cloned.1.call-done) | data formatting | bytes 4194304
  (61 shorter events, 6.6 us)
Async XLA Ops:
  7.2 48.5 %reduce-scatter.11.cloned.1.call-start = ((), (), s32[]{:S(2)}) async-start(), calls=%async_computation.7 | async-start | bytes 2359296 | tf_op jit(solution)/shard_map/reduce_scatter | solution.py:34
  11.1 89.6 %reduce-scatter.19.cloned.1.call-start = ((), (), s32[]{:S(2)}) async-start(), calls=%async_computation.12 | async-start | bytes 2359296
  16.2 1.2 copy-start.2
  16.2 2.1 copy-start.3
  16.3 3.0 %copy-start.4 = (f32[1,1024,256]{2,1,0:T(8,128)S(1)}, f32[1,1024,256]{2,1,0:T(8,128)}, u32[]{:S(2)}) copy-start(f32[1,1024,256]{2,1,0:T(8,128)} %param.25) | copy-start | bytes 3145732
  16.3 136.7 %reduce-scatter.13.cloned.1.call-start = ((), (), s32[]{:S(2)}) async-start(), calls=%async_computation.9 | async-start | bytes 589824 | tf_op jit(solution)/shard_map/reduce_scatter | solution.py:40
  18.3 161.3 %reduce-scatter.15.cloned.1.call-start = ((), (), s32[]{:S(2)}) async-start(), calls=%async_computation.10 | async-start | bytes 589824 | tf_op jit(solution)/shard_map/reduce_scatter | solution.py:43
  19.3 198.1 %reduce-scatter.17.cloned.1.call-start = ((), (), s32[]{:S(2)}) async-start(), calls=%async_computation.11 | async-start | bytes 589824 | tf_op jit(solution)/shard_map/reduce_scatter | solution.py:46
  20.2 35.6 %copy-start.5 = (f32[128,1024]{1,0:T(8,128)S(1)}, f32[128,1024]{1,0:T(8,128)}, u32[]{:S(2)}) copy-start(f32[128,1024]{1,0:T(8,128)} %param.28) | copy-start | bytes 1572868
  20.2 35.6 %copy-start.6 = (f32[128,1024]{1,0:T(8,128)S(1)}, f32[128,1024]{1,0:T(8,128)}, u32[]{:S(2)}) copy-start(f32[128,1024]{1,0:T(8,128)} %param.35) | copy-start | bytes 1572868
  20.2 234.8 %reduce-scatter.21.cloned.1.call-start = ((), (), s32[]{:S(2)}) async-start(), calls=%async_computation.13 | async-start | bytes 589824
  22.6 79.2 %copy-start.7 = (f32[1024,128]{1,0:T(8,128)S(1)}, f32[1024,128]{1,0:T(8,128)}, u32[]{:S(2)}) copy-start(f32[1024,128]{1,0:T(8,128)} %param.29) | copy-start | bytes 1572868
  22.6 79.2 %copy-start.8 = (f32[1024,128]{1,0:T(8,128)S(1)}, f32[1024,128]{1,0:T(8,128)}, u32[]{:S(2)}) copy-start(f32[1024,128]{1,0:T(8,128)} %param.36) | copy-start | bytes 1572868
  22.7 262.0 %all-gather.3.cloned.1.call-start = ((), (), s32[]{:S(2)}) async-start(), calls=%async_computation.8 | async-start | bytes 2359296 | tf_op jit(solution)/shard_map/all_gather | solution.py:81
  104.6 3.8 %copy-start.16 = (f32[1,1024]{1,0:T(1,128)S(1)}, f32[1,1024]{1,0:T(1,128)}, u32[]{:S(2)}) copy-start(f32[1,1024]{1,0:T(1,128)} %param.27) | copy-start | bytes 12292
  104.6 38.3 %copy-start.17 = (f32[128]{0:T(128)S(1)}, f32[128]{0:T(128)}, u32[]{:S(2)}) copy-start(f32[128]{0:T(128)} %param.34) | copy-start | bytes 1540
  104.6 38.3 %copy-start.18 = (f32[128]{0:T(128)S(1)}, f32[128]{0:T(128)}, u32[]{:S(2)}) copy-start(f32[128]{0:T(128)} %param.41) | copy-start | bytes 1540
  104.6 48.4 %copy-start.9 = (f32[128,256]{1,0:T(8,128)S(1)}, f32[128,256]{1,0:T(8,128)}, u32[]{:S(2)}) copy-start(f32[128,256]{1,0:T(8,128)} %param.30) | copy-start | bytes 393220
  104.6 48.4 %copy-start.10 = (f32[128,256]{1,0:T(8,128)S(1)}, f32[128,256]{1,0:T(8,128)}, u32[]{:S(2)}) copy-start(f32[128,256]{1,0:T(8,128)} %param.37) | copy-start | bytes 393220
  104.6 75.1 %copy-start.11 = (f32[128,256]{1,0:T(8,128)S(1)}, f32[128,256]{1,0:T(8,128)}, u32[]{:S(2)}) copy-start(f32[128,256]{1,0:T(8,128)} %param.31) | copy-start | bytes 393220
  104.6 75.1 %copy-start.12 = (f32[128,256]{1,0:T(8,128)S(1)}, f32[128,256]{1,0:T(8,128)}, u32[]{:S(2)}) copy-start(f32[128,256]{1,0:T(8,128)} %param.38) | copy-start | bytes 393220
  104.6 163.9 %all-to-all-start = ((bf16[8,1024,128]{2,1,0:T(8,128)(2,1)}), bf16[8,1024,128]{2,1,0:T(8,128)(2,1)S(1)}, u32[]{:S(2)}, u32[]{:S(2)}) async-start(bf16[8,1024,128]{2,1,0:T(8,128)(2,1)} %stack.2), calls=%async_computation.1 | async-start | bytes 4194304 | tf_op jit(solution)/shard_map/all_to_all | solution.py:83
  108.4 109.0 %copy-start.13 = (f32[128,256]{1,0:T(8,128)S(1)}, f32[128,256]{1,0:T(8,128)}, u32[]{:S(2)}) copy-start(f32[128,256]{1,0:T(8,128)} %param.32) | copy-start | bytes 393220
  108.4 108.9 %copy-start.14 = (f32[128,256]{1,0:T(8,128)S(1)}, f32[128,256]{1,0:T(8,128)}, u32[]{:S(2)}) copy-start(f32[128,256]{1,0:T(8,128)} %param.39) | copy-start | bytes 393220
  108.4 147.6 %copy-start.15 = (f32[256,128]{1,0:T(8,128)S(1)}, f32[256,128]{1,0:T(8,128)}, u32[]{:S(2)}) copy-start(f32[256,128]{1,0:T(8,128)} %param.33) | copy-start | bytes 393220
  287.8 1.6 copy-start
  287.8 2.4 copy-start.1
Sparse Core Ops, SparseCore 0:
  11.9 43.8 reduce-scatter.10
  59.6 41.0 reduce-scatter.18
  104.4 37.5 reduce-scatter.12
  145.5 34.0 reduce-scatter.14
  183.1 34.1 reduce-scatter.16
  220.8 34.1 reduce-scatter.20
  256.9 27.7 all-gather.2
